TPU v7x, 32 devices: a whole 2x2x4 slice. The times are simulated.
32 devices in a mesh: rep: 2 (over y), seq: 4 (over z), head: 4 (over x, core).
Axes of the slice: x: 2, y: 2, z: 4, core: 2. Of those that a mesh axis runs over, the one named last changes fastest.
Arguments:
- queries: bfloat16 [2048, 4096], P(('rep', 'seq'), 'head'), parts along dimension 0, may hold values from -520 to 520
- rotated_key_states: bfloat16 [2048, 1024], P(('rep', 'seq'), 'head'), parts along dimension 0, may hold values from -6 to 6
- value_state_array: bfloat16 [2048, 1024], P(('rep', 'seq'), 'head'), parts along dimension 0, may hold values from -6 to 6
- residual: bfloat16 [2048, 4096], P(('rep', 'seq'), 'head'), parts along dimension 0, may hold values from -60 to 60
- out_weight: bfloat16 [4096, 4096], P('head'), may hold values from -0.75 to 0.75
- norm_gain: bfloat16 [4096], P('head'), may hold values from 0.5 to 1.5
- block_order: int32 [16], P('rep'), parts along dimension 0, may hold values from 0 to 7, as said below
Outputs:
- normed: bfloat16 [2048, 4096], P(('rep', 'seq'), 'head'), parts along dimension 0
There are 2 independent parts, one for each index of `rep`. A program takes and returns all parts, laid end to end along the dimension named above; an argument that names none is the same for every part. Nothing has to cross between parts.
Inputs may be any that keep to these rules, and one draw needn't show every extreme that they name: `block_order`: slots 2i and 2i + 1 hold blocks c and 7 - c in either order; every block appears once.
All inputs are finite; a program needn't handle non-finite values.
Results may differ from a plain program's by a relative error of at most 0.008.
Values may be sent and summed in bfloat16 or wider, within the bound.
A program may use at most 64 MiB of HBM per device.

v0:
```python
import functools
import math

import jax
import jax.numpy as jnp
from jax import lax
from jax.experimental import pallas as pl
from jax.experimental.pallas import tpu as pltpu
from jax.sharding import PartitionSpec as P

MESH = pl.DeviceIdType.MESH
HEAD_SIZE = 128
NORM_EPSILON = 1e-05
MASKED = -1e30


def kernel(
    ns, nh, order_ref, k_hbm, v_hbm, gain_hbm, q_hbm, res_hbm, w_hbm, out_ref,
    k_ref, v_ref, gain_ref, q_vm, res_vm, q_stack, w_own, w_peer, kv, att, peer_att, part, part_in,
    ssq, ssq_in, acc, peak, denom, mixed, ahead,
    load_sem, local_sem, kv_send, kv_recv, w_send, w_recv, att_send, att_recv,
    part_send, part_recv, ssq_send, ssq_recv,
):
    seq, head = lax.axis_index("seq"), lax.axis_index("head")
    rows, width = q_vm.shape
    block = rows // 2
    kv_heads = k_ref.shape[1] // HEAD_SIZE
    group = width // k_ref.shape[1]
    features = res_vm.shape[1]
    pairs = nh // 2
    bit, pair = lax.rem(head, 2), head // 2
    sibling = head + 1 - 2 * bit
    keys = ns * block

    barrier = pltpu.get_barrier_semaphore()

    @pl.when(seq > 0)
    def _():
        pl.semaphore_signal(barrier, inc=1, device_id={"seq": seq - 1}, device_id_type=MESH)

    @pl.when(seq < ns - 1)
    def _():
        pl.semaphore_signal(barrier, inc=1, device_id={"seq": seq + 1}, device_id_type=MESH)

    for step in range(1, nh):
        pl.semaphore_signal(
            barrier, inc=1, device_id={"head": lax.rem(head + step, nh)}, device_id_type=MESH
        )
    q_copy = pltpu.make_async_copy(q_hbm, q_vm, local_sem.at[0])
    res_copy = pltpu.make_async_copy(res_hbm, res_vm, local_sem.at[1])
    loads = [
        pltpu.make_async_copy(source, target, load_sem.at[i])
        for i, (source, target) in enumerate(((k_hbm, k_ref), (v_hbm, v_ref), (gain_hbm, gain_ref)))
    ]
    for load in loads:
        load.start()
    q_copy.start()

    first, second = order_ref[2 * seq], order_ref[2 * seq + 1]
    early_id, late_id = jnp.minimum(first, second), jnp.maximum(first, second)
    swapped = jnp.where(first > second, 1, 0)

    def halves(ref):
        low, high = ref[:block, :].astype(jnp.float32), ref[block:, :].astype(jnp.float32)
        swap = jnp.full(low.shape, swapped, jnp.int32) != 0
        return jnp.where(swap, high, low), jnp.where(swap, low, high)

    for index, ref in ((0, k_ref), (1, v_ref)):
        loads[index].wait()
        early, late = halves(ref)
        kv[index, seq] = early.astype(jnp.bfloat16)
        kv[2 + index, seq] = late.astype(jnp.bfloat16)

    near = jnp.where(seq > 0, 1, 0) + jnp.where(seq < ns - 1, 1, 0)
    pl.semaphore_wait(barrier, near + nh - 1)

    def kv_copy(direction, chunk, distance):
        piece = seq - distance if direction == 0 else seq + distance
        target = seq + 1 if direction == 0 else seq - 1
        return pltpu.make_async_remote_copy(
            src_ref=kv.at[chunk, piece],
            dst_ref=kv.at[chunk, piece],
            send_sem=kv_send.at[direction, chunk, distance],
            recv_sem=kv_recv.at[chunk, piece],
            device_id={"seq": target},
            device_id_type=MESH,
        )

    def sends(direction, distance):
        if direction == 0:
            return jnp.logical_and(seq >= distance, seq < ns - 1)
        return jnp.logical_and(seq + distance <= ns - 1, seq > 0)

    def arrives(direction, distance):
        return seq >= distance if direction == 0 else seq + distance <= ns - 1

    def start_kv(chunk, distance):
        for direction in range(2):
            @pl.when(sends(direction, distance))
            def _():
                kv_copy(direction, chunk, distance).start()

    def forward_kv(chunk, distance):
        for direction in range(2):
            @pl.when(sends(direction, distance))
            def _():
                kv_copy(direction, chunk, distance).wait_recv()
                kv_copy(direction, chunk, distance).start()

    def collect_kv(chunks, distances):
        for distance in distances:
            for chunk in chunks:
                for direction in range(2):
                    @pl.when(
                        jnp.logical_and(
                            arrives(direction, distance),
                            jnp.logical_not(sends(direction, distance)),
                        )
                    )
                    def _():
                        kv_copy(direction, chunk, distance).wait_recv()

    for chunk in (0, 1, 2):
        start_kv(chunk, 0)

    def w_copies(index):
        mine = pl.ds(pl.multiple_of((2 * index + bit) * features, 128), features)
        theirs = pl.ds(pl.multiple_of((2 * index + 1 - bit) * features, 128), features)
        local = pltpu.make_async_copy(w_hbm.at[:, mine], w_own.at[index], local_sem.at[2 + index])
        remote = pltpu.make_async_remote_copy(
            src_ref=w_hbm.at[:, theirs],
            dst_ref=w_peer.at[index],
            send_sem=w_send.at[index],
            recv_sem=w_recv.at[index],
            device_id={"head": sibling},
            device_id_type=MESH,
        )
        return local, remote

    for index in range(pairs):
        local, remote = w_copies(index)
        remote.start()
        local.start()
    res_copy.start()

    q_copy.wait()
    for side, part_rows in enumerate(halves(q_vm)):
        part_rows = part_rows.astype(jnp.bfloat16)
        for h in range(kv_heads * group):
            q_stack[side, h // group, (h % group) * block:(h % group + 1) * block, :] = part_rows[
                :, h * HEAD_SIZE:(h + 1) * HEAD_SIZE
            ]

    for distance in range(1, ns - 1):
        for chunk in (0, 1):
            forward_kv(chunk, distance)
    start_kv(3, 0)
    collect_kv((0, 1), range(1, ns))

    chunk_blocks = math.gcd(ns, 4)
    factor = math.log2(math.e) * HEAD_SIZE ** -0.5
    stack = group * block

    def attend(state, q, g, late, masked, own_id, at, blocks):
        chunk_keys = blocks * block
        lanes = slice(g * HEAD_SIZE, (g + 1) * HEAD_SIZE)
        base = 2 if late else 0
        k = kv[base, pl.ds(at, blocks), :, lanes].reshape(chunk_keys, HEAD_SIZE)
        v = kv[base + 1, pl.ds(at, blocks), :, lanes].reshape(chunk_keys, HEAD_SIZE)
        scores = lax.dot_general(
            q, k, (((1,), (1,)), ((), ())), preferred_element_type=jnp.float32
        ) * factor
        if masked:
            starts = []
            for j in range(blocks):
                a, b = order_ref[2 * (at + j)], order_ref[2 * (at + j) + 1]
                there = jnp.maximum(a, b) if late else jnp.minimum(a, b)
                gap = (own_id - there) * block
                lane = lax.broadcasted_iota(jnp.int32, (block, block), 1)
                row = lax.broadcasted_iota(jnp.int32, (block, block), 0)
                starts.append(jnp.where(lane - row <= gap, 0.0, MASKED))
            bias = starts[0] if blocks == 1 else jnp.concatenate(starts, axis=1)
            scores = (scores.reshape(group, block, chunk_keys) + bias[None]).reshape(
                stack, chunk_keys
            )
        top = jnp.max(scores, axis=1, keepdims=True)
        if state is None:
            weights = jnp.exp2(scores - top)
            total = jnp.sum(weights, axis=1, keepdims=True)
            value = jnp.dot(weights.astype(jnp.bfloat16), v, preferred_element_type=jnp.float32)
            return top, total, value
        old_top, old_total, old_value = state
        top = jnp.maximum(old_top, top)
        weights = jnp.exp2(scores - top)
        scale = jnp.exp2(old_top - top)
        total = old_total * scale + jnp.sum(weights, axis=1, keepdims=True)
        value = old_value * scale + jnp.dot(
            weights.astype(jnp.bfloat16), v, preferred_element_type=jnp.float32
        )
        return top, total, value

    def attend_all(state, q, g, late, masked, own_id):
        if ns == chunk_blocks:
            return attend(state, q, g, late, masked, own_id, 0, ns)
        if state is None:
            state = (
                jnp.full((stack, 1), MASKED, jnp.float32),
                jnp.zeros((stack, 1), jnp.float32),
                jnp.zeros((stack, HEAD_SIZE), jnp.float32),
            )
        return lax.fori_loop(
            0,
            ns // chunk_blocks,
            lambda i, s: attend(
                s, q, g, late, masked, own_id, i * chunk_blocks, chunk_blocks
            ),
            state,
        )

    def store_attention(side, g, state):
        _, total, value = state
        result = (value / total).astype(jnp.bfloat16)
        for h in range(group):
            column = (g * group + h) * HEAD_SIZE
            att[side, :, column:column + HEAD_SIZE] = result[h * block:(h + 1) * block, :]

    def att_copy(side, g):
        lanes = slice(g * group * HEAD_SIZE, (g + 1) * group * HEAD_SIZE)
        return pltpu.make_async_remote_copy(
            src_ref=att.at[side, :, lanes],
            dst_ref=peer_att.at[side, :, lanes],
            send_sem=att_send.at[side, g],
            recv_sem=att_recv.at[side, g],
            device_id={"head": sibling},
            device_id_type=MESH,
        )

    pieces = features // math.gcd(features, 256)
    piece_width = features // pieces

    def part_copy(side, step, piece):
        return pltpu.make_async_remote_copy(
            src_ref=part.at[side, step - 1, piece],
            dst_ref=part_in.at[side, step - 1, piece],
            send_sem=part_send.at[side, step - 1, piece],
            recv_sem=part_recv.at[side, step - 1, piece],
            device_id={"head": 2 * lax.rem(pair + step, pairs) + bit},
            device_id_type=MESH,
        )

    def own_part(side, owner, columns):
        return jnp.dot(att[side], w_own[owner, :, columns], preferred_element_type=jnp.float32)

    def peer_part(side, owner, columns):
        return jnp.dot(
            peer_att[side], w_peer[owner, :, columns], preferred_element_type=jnp.float32
        )

    def own_residual(side, columns):
        low = res_vm[:block, columns].astype(jnp.float32)
        high = res_vm[block:, columns].astype(jnp.float32)
        swap = jnp.full(low.shape, swapped, jnp.int32) != 0
        return jnp.where(swap, high, low) if side == 0 else jnp.where(swap, low, high)

    spans = [slice(i * piece_width, (i + 1) * piece_width) for i in range(pieces)]

    def project_side(side):
        owner = lax.rem(pair + 1, pairs)
        for columns in spans:
            ahead[:, columns] = own_part(side, owner, columns)
        for g in range(kv_heads):
            att_copy(side, g).wait_recv()
        for step in range(1, pairs):
            owner = lax.rem(pair + step, pairs)
            for piece, columns in enumerate(spans):
                own = ahead[:, columns] if step == 1 else own_part(side, owner, columns)
                part[side, step - 1, piece] = (own + peer_part(side, owner, columns)).astype(
                    jnp.bfloat16
                )
                part_copy(side, step, piece).start()
        for columns in spans:
            mixed[side, :, columns] = (
                own_part(side, pair, columns)
                + peer_part(side, pair, columns)
                + own_residual(side, columns)
            )

    def ssq_copy(side, step):
        return pltpu.make_async_remote_copy(
            src_ref=ssq.at[side],
            dst_ref=ssq_in.at[side, step - 1],
            send_sem=ssq_send.at[side, step - 1],
            recv_sem=ssq_recv.at[side, step - 1],
            device_id={"head": lax.rem(head + step, nh)},
            device_id_type=MESH,
        )

    def finish_side(side):
        squares = jnp.zeros((block, 128), jnp.float32)
        for piece, columns in enumerate(spans):
            total = mixed[side, :, columns]
            for step in range(1, pairs):
                part_copy(side, step, piece).wait_recv()
                total = total + part_in[side, step - 1, piece].astype(jnp.float32)
            mixed[side, :, columns] = total
            for lane in range(0, piece_width, 128):
                strip = total[:, lane:lane + 128]
                squares = squares + strip * strip
        row_sums = jnp.sum(jnp.transpose(squares), axis=0, keepdims=True)
        ssq[side] = jnp.broadcast_to(row_sums, (8, block))
        for step in range(1, nh):
            ssq_copy(side, step).start()
        mixed[side] = mixed[side] * gain_ref[...].astype(jnp.float32).reshape(1, features)

    def norm_side(side):
        total = ssq[side]
        for step in range(1, nh):
            ssq_copy(side, step).wait_recv()
            total = total + ssq_in[side, step - 1]
        inverse = lax.rsqrt(total / (nh * features) + NORM_EPSILON)
        column = jnp.transpose(jnp.broadcast_to(inverse[:1, :], (128, block)))[:, :1]
        return mixed[side] * column

    def keep_state(g, state):
        top, total, value = state
        acc[g] = value
        peak[g] = jnp.broadcast_to(top, (stack, 128))
        denom[g] = jnp.broadcast_to(total, (stack, 128))

    def kept_state(g):
        return peak[g][:, :1], denom[g][:, :1], acc[g]

    late_steps = list(range(1, ns - 1))
    for g in range(kv_heads):
        store_attention(0, g, attend_all(None, q_stack[0, g], g, False, True, early_id))
        att_copy(0, g).start()
    for g in range(kv_heads):
        keep_state(g, attend_all(None, q_stack[1, g], g, False, False, late_id))
    for distance in late_steps[:1]:
        for chunk in (2, 3):
            forward_kv(chunk, distance)
    for index in range(pairs):
        local, remote = w_copies(index)
        local.wait()
        remote.wait_recv()
    res_copy.wait()
    loads[2].wait()
    project_side(0)
    for distance in late_steps[1:]:
        for chunk in (2, 3):
            forward_kv(chunk, distance)
    split = ns == chunk_blocks and ns > 1
    if split:
        lower = seq < ns // 2
        begin, far = jnp.where(lower, 0, 1), jnp.where(lower, ns - 1, 0)
        collect_kv((2, 3), range(1, ns - 1))
        for g in range(kv_heads):
            keep_state(
                g, attend(kept_state(g), q_stack[1, g], g, True, True, late_id, begin, ns - 1)
            )
    collect_kv((2, 3), range(ns - 1, ns) if split else range(1, ns))
    for g in range(kv_heads):
        if split:
            state = attend(kept_state(g), q_stack[1, g], g, True, True, late_id, far, 1)
        else:
            state = attend_all(kept_state(g), q_stack[1, g], g, True, True, late_id)
        store_attention(1, g, state)
        att_copy(1, g).start()
    project_side(1)
    finish_side(0)
    mixed[0] = norm_side(0)
    finish_side(1)
    early_out, late_out = mixed[0], norm_side(1)
    swap = jnp.full(early_out.shape, swapped, jnp.int32) != 0
    out_ref[:block, :] = jnp.where(swap, late_out, early_out).astype(jnp.bfloat16)
    out_ref[block:, :] = jnp.where(swap, early_out, late_out).astype(jnp.bfloat16)

    for chunk in range(4):
        for distance in range(ns - 1):
            for direction in range(2):
                @pl.when(sends(direction, distance))
                def _():
                    kv_copy(direction, chunk, distance).wait_send()
    for index in range(pairs):
        w_copies(index)[1].wait_send()
    for side in range(2):
        for g in range(kv_heads):
            att_copy(side, g).wait_send()
        for step in range(1, pairs):
            for piece in range(pieces):
                part_copy(side, step, piece).wait_send()
        for step in range(1, nh):
            ssq_copy(side, step).wait_send()


def body(ns, nh, queries, keys, values, residual, weight, gain, order):
    rows, width = queries.shape
    block, kv_width = rows // 2, keys.shape[1]
    kv_heads = kv_width // HEAD_SIZE
    stack = (width // kv_width) * block
    features = residual.shape[1]
    pairs = nh // 2
    others = max(pairs - 1, 1)
    pieces = features // math.gcd(features, 256)
    vmem, hbm = pl.BlockSpec(memory_space=pltpu.VMEM), pl.BlockSpec(memory_space=pl.ANY)
    bf16, f32, dma = jnp.bfloat16, jnp.float32, pltpu.SemaphoreType.DMA
    return pl.pallas_call(
        functools.partial(kernel, ns, nh),
        out_shape=jax.ShapeDtypeStruct((rows, features), bf16),
        in_specs=[pl.BlockSpec(memory_space=pltpu.SMEM)] + [hbm] * 6,
        out_specs=vmem,
        scratch_shapes=[
            pltpu.VMEM((rows, kv_width), bf16),
            pltpu.VMEM((rows, kv_width), bf16),
            pltpu.VMEM((features,), bf16),
            pltpu.VMEM((rows, width), bf16),
            pltpu.VMEM((rows, features), bf16),
            pltpu.VMEM((2, kv_heads, stack, HEAD_SIZE), bf16),
            pltpu.VMEM((pairs, width, features), bf16),
            pltpu.VMEM((pairs, width, features), bf16),
            pltpu.VMEM((4, ns, block, kv_width), bf16),
            pltpu.VMEM((2, block, width), bf16),
            pltpu.VMEM((2, block, width), bf16),
            pltpu.VMEM((2, others, pieces, block, features // pieces), bf16),
            pltpu.VMEM((2, others, pieces, block, features // pieces), bf16),
            pltpu.VMEM((2, 8, block), f32),
            pltpu.VMEM((2, nh - 1, 8, block), f32),
            pltpu.VMEM((kv_heads, stack, HEAD_SIZE), f32),
            pltpu.VMEM((kv_heads, stack, 128), f32),
            pltpu.VMEM((kv_heads, stack, 128), f32),
            pltpu.VMEM((2, block, features), f32),
            pltpu.VMEM((block, features), f32),
            dma((3,)),
            dma((2 + pairs,)),
            dma((2, 4, ns)),
            dma((4, ns)),
            dma((pairs,)),
            dma((pairs,)),
            dma((2, kv_heads)),
            dma((2, kv_heads)),
            dma((2, others, pieces)),
            dma((2, others, pieces)),
            dma((2, nh - 1)),
            dma((2, nh - 1)),
        ],
        compiler_params=pltpu.CompilerParams(
            collective_id=0, has_side_effects=True, vmem_limit_bytes=60 * 1024 * 1024
        ),
    )(order, keys, values, gain, queries, residual, weight)


def solution(mesh):
    in_specs = (
        P(("rep", "seq"), "head"),
        P(("rep", "seq"), "head"),
        P(("rep", "seq"), "head"),
        P(("rep", "seq"), "head"),
        P("head", None),
        P("head"),
        P("rep"),
    )
    out_specs = P(("rep", "seq"), "head")
    ns, nh = mesh.shape["seq"], mesh.shape["head"]
    return jax.shard_map(
        functools.partial(body, ns, nh),
        mesh=mesh,
        in_specs=in_specs,
        out_specs=out_specs,
        check_vma=False,
    )
```

profile of v0, /device:TPU:0, one launch (start us, length us, event | category | flops | bytes accessed | tf_op | source)
XLA Modules:
  0.0 41.6 jit_solution(11601240367137276413)
XLA Ops:
  0.0 39.7 %shard_map.73 = bf16[256,1024]{1,0:T(8,128)(2,1)} custom-call(s32[8]{0:T(128)} %order_ref.1, bf16[256,256]{1,0:T(8,128)(2,1)} %k_hbm.1, bf16[256,256]{1,0:T(8,128)(2,1)} %v_hbm.1, bf16[1024]{0:T(1024)(128)(2,1)} %gain_hbm.1, bf16[256,1024]{1,0:T(8,128)(2,1)} %q_hbm.1, bf16[256,1024]{1,0:T(8,128)(2,1)} %res_hbm.1, bf16[1024,4096]{1,0:T(8,128)(2,1)} %w_hbm.1), custom_call_target="tpu_custom_call" | custom-call | tf_op jit(solution)/shard_map/pallas_call | solution.py:407
  39.7 1.9 %copy.9 = bf16[256,1024]{1,0:T(8,128)(2,1)} copy(bf16[256,1024]{1,0:T(8,128)(2,1)} %shard_map.73) | data formatting | bytes 1048576
where the time goes:
time: 41.8 us; the launch traced here: 41.6 us
  Pallas kernels  39.7 us (95%)
  local copies, waits for them, and re-layouts  1.87 us (4%)
    pallas_call x1, Pallas kernels, body(): pl.pallas_call(functools.partial(kernel, ns, nh), out_shape=jax.ShapeDtyp...  39.7 us
    unnamed x1, local copies, waits for them, and re-layouts  1.87 us

commit v1 on v0

--- a/solution.py
+++ b/solution.py
@@ -444,9 +444,9 @@
             dma((2, nh - 1)),
         ],
         compiler_params=pltpu.CompilerParams(
-            collective_id=0, has_side_effects=True, vmem_limit_bytes=60 * 1024 * 1024
+            collective_id=0, has_side_effects=True, vmem_limit_bytes=40 * 1024 * 1024
         ),
-    )(order, keys, values, gain, queries, residual, weight)
+    )(*[pltpu.with_memory_space_constraint(a, pltpu.HBM) for a in (order, keys, values, gain, queries, residual, weight)])
 
 
 def solution(mesh):

time: 41.8 us -> 39.9 us (0.955)
  local copies, waits for them, and re-layouts: 1.87 us -> 0.8 us
  Pallas kernels: 39.7 us -> 38.9 us
    unnamed x1, local copies, waits for them, and re-layouts: 1.87 us -> 0.8 us
    pallas_call x1, Pallas kernels: 39.7 us -> 38.9 us  [body(): pl.pallas_call(functools.partial(kernel, ns, nh), out_shape=jax.ShapeDtyp...]
where the time goes in v1:
time: 39.9 us; the launch traced here: 39.7 us
  Pallas kernels  38.9 us (97%)
  local copies, waits for them, and re-layouts  0.8 us (2%)
    pallas_call x1, Pallas kernels, body(): pl.pallas_call(functools.partial(kernel, ns, nh), out_shape=jax.ShapeDtyp...  38.9 us

profile of v1, /device:TPU:0, one launch (start us, length us, event | category | flops | bytes accessed | tf_op | source)
XLA Modules:
  0.0 39.7 jit_solution(14695913882902487568)
XLA Ops:
  0.0 38.9 %shard_map.73 = bf16[256,1024]{1,0:T(8,128)(2,1)S(1)} custom-call(s32[8]{0:T(128)} %order_ref.1, bf16[256,256]{1,0:T(8,128)(2,1)} %k_hbm.1, bf16[256,256]{1,0:T(8,128)(2,1)} %v_hbm.1, bf16[1024]{0:T(1024)(128)(2,1)} %gain_hbm.1, bf16[256,1024]{1,0:T(8,128)(2,1)} %q_hbm.1, bf16[256,1024]{1,0:T(8,128)(2,1)} %res_hbm.1, bf16[1024,4096]{1,0:T(8,128)(2,1)} %w_hbm.1), custom_call_target="tpu_custom_call" | custom-call | tf_op jit(solution)/shard_map/pallas_call | solution.py:407
  38.9 0.8 %copy.9 = bf16[256,1024]{1,0:T(8,128)(2,1)} copy(bf16[256,1024]{1,0:T(8,128)(2,1)S(1)} %shard_map.73) | data formatting | bytes 1048576

commit v2 on v1

--- a/solution.py
+++ b/solution.py
@@ -15,10 +15,10 @@
 
 
 def kernel(
-    ns, nh, order_ref, k_hbm, v_hbm, gain_hbm, q_hbm, res_hbm, w_hbm, out_ref,
-    k_ref, v_ref, gain_ref, q_vm, res_vm, q_stack, w_own, w_peer, kv, att, peer_att, part, part_in,
-    ssq, ssq_in, acc, peak, denom, mixed, ahead,
-    load_sem, local_sem, kv_send, kv_recv, w_send, w_recv, att_send, att_recv,
+    ns, nh, order_hbm, k_hbm, v_hbm, gain_hbm, q_hbm, res_hbm, w_hbm, out_ref,
+    order_ref, k_ref, v_ref, gain_ref, q_vm, res_vm, q_stack, w_own, w_peer, kv, att, peer_att, part, part_in,
+    ssq, ssq_in, acc, peak, denom, mixed, ahead, peer_kv,
+    load_sem, local_sem, kv_send, kv_recv, peer_send, peer_recv, relay_send, w_send, w_recv, att_send, att_recv,
     part_send, part_recv, ssq_send, ssq_recv,
 ):
     seq, head = lax.axis_index("seq"), lax.axis_index("head")
@@ -32,7 +32,12 @@
     sibling = head + 1 - 2 * bit
     keys = ns * block
 
+    def drain(ref, sem):
+        pltpu.make_async_copy(ref, ref, sem).wait()
+
     barrier = pltpu.get_barrier_semaphore()
+
+    near = jnp.where(seq > 0, 1, 0) + jnp.where(seq < ns - 1, 1, 0)
 
     @pl.when(seq > 0)
     def _():
@@ -42,10 +47,22 @@
     def _():
         pl.semaphore_signal(barrier, inc=1, device_id={"seq": seq + 1}, device_id_type=MESH)
 
+    for offset in (-1, 1):
+        @pl.when(jnp.logical_and(bit == 1, jnp.logical_and(seq + offset >= 0, seq + offset < ns)))
+        def _():
+            pl.semaphore_signal(
+                barrier,
+                inc=1,
+                device_id={"seq": seq + offset, "head": sibling},
+                device_id_type=MESH,
+            )
+
     for step in range(1, nh):
         pl.semaphore_signal(
             barrier, inc=1, device_id={"head": lax.rem(head + step, nh)}, device_id_type=MESH
         )
+    order_copy = pltpu.make_async_copy(order_hbm, order_ref, load_sem.at[3])
+    order_copy.start()
     q_copy = pltpu.make_async_copy(q_hbm, q_vm, local_sem.at[0])
     res_copy = pltpu.make_async_copy(res_hbm, res_vm, local_sem.at[1])
     loads = [
@@ -56,6 +73,7 @@
         load.start()
     q_copy.start()
 
+    order_copy.wait()
     first, second = order_ref[2 * seq], order_ref[2 * seq + 1]
     early_id, late_id = jnp.minimum(first, second), jnp.maximum(first, second)
     swapped = jnp.where(first > second, 1, 0)
@@ -71,8 +89,7 @@
         kv[index, seq] = early.astype(jnp.bfloat16)
         kv[2 + index, seq] = late.astype(jnp.bfloat16)
 
-    near = jnp.where(seq > 0, 1, 0) + jnp.where(seq < ns - 1, 1, 0)
-    pl.semaphore_wait(barrier, near + nh - 1)
+    pl.semaphore_wait(barrier, near * (2 - bit) + nh - 1)
 
     def kv_copy(direction, chunk, distance):
         piece = seq - distance if direction == 0 else seq + distance
@@ -80,7 +97,7 @@
         return pltpu.make_async_remote_copy(
             src_ref=kv.at[chunk, piece],
             dst_ref=kv.at[chunk, piece],
-            send_sem=kv_send.at[direction, chunk, distance],
+            send_sem=kv_send.at[direction, distance],
             recv_sem=kv_recv.at[chunk, piece],
             device_id={"seq": target},
             device_id_type=MESH,
@@ -94,53 +111,139 @@
     def arrives(direction, distance):
         return seq >= distance if direction == 0 else seq + distance <= ns - 1
 
-    def start_kv(chunk, distance):
-        for direction in range(2):
-            @pl.when(sends(direction, distance))
+    def cross_copy(direction, chunk):
+        return pltpu.make_async_remote_copy(
+            src_ref=kv.at[chunk, seq],
+            dst_ref=peer_kv.at[chunk, seq],
+            send_sem=kv_send.at[direction, 0],
+            recv_sem=peer_recv.at[chunk, seq],
+            device_id={"seq": seq + 1 if direction == 0 else seq - 1, "head": sibling},
+            device_id_type=MESH,
+        )
+
+    def peer_copy(direction, chunk, distance, origin=None):
+        origin = distance if origin is None else origin
+        piece = seq - origin if direction == 0 else seq + origin
+        return pltpu.make_async_remote_copy(
+            src_ref=peer_kv.at[chunk, piece],
+            dst_ref=peer_kv.at[chunk, piece],
+            send_sem=peer_send.at[direction, distance - 1],
+            recv_sem=peer_recv.at[chunk, piece],
+            device_id={"seq": seq + 1 if direction == 0 else seq - 1},
+            device_id_type=MESH,
+        )
+
+    def landed(direction, chunk, distance):
+        return peer_copy(direction, chunk, min(distance, max(ns - 2, 1)), distance)
+
+    def relay_copy(direction, chunk, distance):
+        piece = seq - distance if direction == 0 else seq + distance
+        return pltpu.make_async_remote_copy(
+            src_ref=peer_kv.at[chunk, piece],
+            dst_ref=kv.at[chunk, piece],
+            send_sem=relay_send,
+            recv_sem=kv_recv.at[chunk, piece],
+            device_id={"head": sibling},
+            device_id_type=MESH,
+        )
+
+    def start_kv(chunk):
+        for direction in (1, 0):
+            @pl.when(sends(direction, 0))
             def _():
-                kv_copy(direction, chunk, distance).start()
-
-    def forward_kv(chunk, distance):
-        for direction in range(2):
-            @pl.when(sends(direction, distance))
+                if chunk < 2:
+                    @pl.when(bit == 0)
+                    def _():
+                        cross_copy(direction, chunk).start()
+
+                    @pl.when(bit == 1)
+                    def _():
+                        kv_copy(direction, chunk, 0).start()
+                else:
+                    kv_copy(direction, chunk, 0).start()
+
+    def passes(direction, chunk, distance):
+        if distance >= ns - 1:
+            return None
+        condition = sends(direction, distance)
+        return jnp.logical_and(condition, bit == 1) if chunk < 2 else condition
+
+    def beside(direction):
+        return seq == (1 if direction == 0 else ns - 2)
+
+    def forward_kv(chunk, distance, edges=None):
+        for direction in (1, 0):
+            condition = passes(direction, chunk, distance)
+            if edges is not None:
+                chosen = beside(direction) if edges else jnp.logical_not(beside(direction))
+                condition = jnp.logical_and(condition, chosen)
+
+            @pl.when(condition)
             def _():
                 kv_copy(direction, chunk, distance).wait_recv()
                 kv_copy(direction, chunk, distance).start()
 
+    def relay_kv(chunk, distance):
+        for direction in (1, 0):
+            @pl.when(jnp.logical_and(bit == 1, arrives(direction, distance)))
+            def _():
+                landed(direction, chunk, distance).wait_recv()
+                if distance < ns - 1:
+                    @pl.when(sends(direction, distance))
+                    def _():
+                        peer_copy(direction, chunk, distance).start()
+                relay_copy(direction, chunk, distance).start()
+
     def collect_kv(chunks, distances):
         for distance in distances:
             for chunk in chunks:
-                for direction in range(2):
-                    @pl.when(
-                        jnp.logical_and(
-                            arrives(direction, distance),
-                            jnp.logical_not(sends(direction, distance)),
-                        )
-                    )
+                for direction in (1, 0):
+                    condition = arrives(direction, distance)
+                    passed = passes(direction, chunk, distance)
+                    if passed is not None:
+                        condition = jnp.logical_and(condition, jnp.logical_not(passed))
+
+                    @pl.when(condition)
                     def _():
                         kv_copy(direction, chunk, distance).wait_recv()
 
+    edge = jnp.logical_or(seq == 0, seq == ns - 1)
     for chunk in (0, 1, 2):
-        start_kv(chunk, 0)
-
-    def w_copies(index):
+        start_kv(chunk)
+
+    @pl.when(edge)
+    def _():
+        start_kv(3)
+
+    def w_local(index):
         mine = pl.ds(pl.multiple_of((2 * index + bit) * features, 128), features)
+        return pltpu.make_async_copy(w_hbm.at[:, mine], w_own.at[index], local_sem.at[2])
+
+    slices = 4
+    depth = width // slices
+
+    def w_remote(number):
+        index, rows_from = number // slices, number % slices * depth
         theirs = pl.ds(pl.multiple_of((2 * index + 1 - bit) * features, 128), features)
-        local = pltpu.make_async_copy(w_hbm.at[:, mine], w_own.at[index], local_sem.at[2 + index])
-        remote = pltpu.make_async_remote_copy(
-            src_ref=w_hbm.at[:, theirs],
-            dst_ref=w_peer.at[index],
-            send_sem=w_send.at[index],
-            recv_sem=w_recv.at[index],
+        return pltpu.make_async_remote_copy(
+            src_ref=w_hbm.at[rows_from:rows_from + depth, theirs],
+            dst_ref=w_peer.at[index, rows_from:rows_from + depth, :],
+            send_sem=w_send,
+            recv_sem=w_recv,
             device_id={"head": sibling},
             device_id_type=MESH,
         )
-        return local, remote
+
+    w_pieces = list(range(pairs * slices))
+    at_once = 2
+
+    def w_next(count):
+        for _ in range(min(count, len(w_pieces))):
+            w_remote(w_pieces.pop(0)).start()
 
     for index in range(pairs):
-        local, remote = w_copies(index)
-        remote.start()
-        local.start()
+        w_local(index).start()
+    w_next(at_once)
     res_copy.start()
 
     q_copy.wait()
@@ -151,22 +254,30 @@
                 :, h * HEAD_SIZE:(h + 1) * HEAD_SIZE
             ]
 
-    for distance in range(1, ns - 1):
+    for distance in range(1, ns):
         for chunk in (0, 1):
-            forward_kv(chunk, distance)
-    start_kv(3, 0)
+            relay_kv(chunk, distance)
+            if distance < ns - 1:
+                forward_kv(chunk, distance)
+            w_next(1)
+        if distance == max(ns - 2, 1):
+            @pl.when(jnp.logical_not(edge))
+            def _():
+                start_kv(3)
+    if ns > 2:
+        for chunk in (2, 3):
+            forward_kv(chunk, 1, edges=True)
+    w_next(len(w_pieces))
     collect_kv((0, 1), range(1, ns))
 
     chunk_blocks = math.gcd(ns, 4)
     factor = math.log2(math.e) * HEAD_SIZE ** -0.5
     stack = group * block
 
-    def attend(state, q, g, late, masked, own_id, at, blocks):
+    def weigh(state, q, g, late, masked, own_id, at, blocks):
         chunk_keys = blocks * block
         lanes = slice(g * HEAD_SIZE, (g + 1) * HEAD_SIZE)
-        base = 2 if late else 0
-        k = kv[base, pl.ds(at, blocks), :, lanes].reshape(chunk_keys, HEAD_SIZE)
-        v = kv[base + 1, pl.ds(at, blocks), :, lanes].reshape(chunk_keys, HEAD_SIZE)
+        k = kv[2 if late else 0, pl.ds(at, blocks), :, lanes].reshape(chunk_keys, HEAD_SIZE)
         scores = lax.dot_general(
             q, k, (((1,), (1,)), ((), ())), preferred_element_type=jnp.float32
         ) * factor
@@ -186,18 +297,24 @@
         top = jnp.max(scores, axis=1, keepdims=True)
         if state is None:
             weights = jnp.exp2(scores - top)
-            total = jnp.sum(weights, axis=1, keepdims=True)
-            value = jnp.dot(weights.astype(jnp.bfloat16), v, preferred_element_type=jnp.float32)
-            return top, total, value
+            return top, jnp.sum(weights, axis=1, keepdims=True), weights.astype(jnp.bfloat16), None
         old_top, old_total, old_value = state
         top = jnp.maximum(old_top, top)
         weights = jnp.exp2(scores - top)
         scale = jnp.exp2(old_top - top)
         total = old_total * scale + jnp.sum(weights, axis=1, keepdims=True)
-        value = old_value * scale + jnp.dot(
-            weights.astype(jnp.bfloat16), v, preferred_element_type=jnp.float32
-        )
-        return top, total, value
+        return top, total, weights.astype(jnp.bfloat16), old_value * scale
+
+    def gather_values(weighed, g, late, at, blocks):
+        top, total, weights, value = weighed
+        lanes = slice(g * HEAD_SIZE, (g + 1) * HEAD_SIZE)
+        v = kv[3 if late else 1, pl.ds(at, blocks), :, lanes].reshape(blocks * block, HEAD_SIZE)
+        fresh = jnp.dot(weights, v, preferred_element_type=jnp.float32)
+        return top, total, fresh if value is None else value + fresh
+
+    def attend(state, q, g, late, masked, own_id, at, blocks):
+        weighed = weigh(state, q, g, late, masked, own_id, at, blocks)
+        return gather_values(weighed, g, late, at, blocks)
 
     def attend_all(state, q, g, late, masked, own_id):
         if ns == chunk_blocks:
@@ -219,7 +336,7 @@
 
     def store_attention(side, g, state):
         _, total, value = state
-        result = (value / total).astype(jnp.bfloat16)
+        result = (value * (1.0 / total)).astype(jnp.bfloat16)
         for h in range(group):
             column = (g * group + h) * HEAD_SIZE
             att[side, :, column:column + HEAD_SIZE] = result[h * block:(h + 1) * block, :]
@@ -229,8 +346,8 @@
         return pltpu.make_async_remote_copy(
             src_ref=att.at[side, :, lanes],
             dst_ref=peer_att.at[side, :, lanes],
-            send_sem=att_send.at[side, g],
-            recv_sem=att_recv.at[side, g],
+            send_sem=att_send,
+            recv_sem=att_recv.at[side],
             device_id={"head": sibling},
             device_id_type=MESH,
         )
@@ -242,7 +359,7 @@
         return pltpu.make_async_remote_copy(
             src_ref=part.at[side, step - 1, piece],
             dst_ref=part_in.at[side, step - 1, piece],
-            send_sem=part_send.at[side, step - 1, piece],
+            send_sem=part_send,
             recv_sem=part_recv.at[side, step - 1, piece],
             device_id={"head": 2 * lax.rem(pair + step, pairs) + bit},
             device_id_type=MESH,
@@ -268,8 +385,7 @@
         owner = lax.rem(pair + 1, pairs)
         for columns in spans:
             ahead[:, columns] = own_part(side, owner, columns)
-        for g in range(kv_heads):
-            att_copy(side, g).wait_recv()
+        drain(peer_att.at[side], att_recv.at[side])
         for step in range(1, pairs):
             owner = lax.rem(pair + step, pairs)
             for piece, columns in enumerate(spans):
@@ -289,8 +405,8 @@
         return pltpu.make_async_remote_copy(
             src_ref=ssq.at[side],
             dst_ref=ssq_in.at[side, step - 1],
-            send_sem=ssq_send.at[side, step - 1],
-            recv_sem=ssq_recv.at[side, step - 1],
+            send_sem=ssq_send,
+            recv_sem=ssq_recv.at[side],
             device_id={"head": lax.rem(head + step, nh)},
             device_id_type=MESH,
         )
@@ -313,9 +429,9 @@
         mixed[side] = mixed[side] * gain_ref[...].astype(jnp.float32).reshape(1, features)
 
     def norm_side(side):
+        drain(ssq_in.at[side], ssq_recv.at[side])
         total = ssq[side]
         for step in range(1, nh):
-            ssq_copy(side, step).wait_recv()
             total = total + ssq_in[side, step - 1]
         inverse = lax.rsqrt(total / (nh * features) + NORM_EPSILON)
         column = jnp.transpose(jnp.broadcast_to(inverse[:1, :], (128, block)))[:, :1]
@@ -338,11 +454,9 @@
         keep_state(g, attend_all(None, q_stack[1, g], g, False, False, late_id))
     for distance in late_steps[:1]:
         for chunk in (2, 3):
-            forward_kv(chunk, distance)
-    for index in range(pairs):
-        local, remote = w_copies(index)
-        local.wait()
-        remote.wait_recv()
+            forward_kv(chunk, distance, edges=False)
+    drain(w_own, local_sem.at[2])
+    drain(w_peer, w_recv)
     res_copy.wait()
     loads[2].wait()
     project_side(0)
@@ -358,39 +472,55 @@
             keep_state(
                 g, attend(kept_state(g), q_stack[1, g], g, True, True, late_id, begin, ns - 1)
             )
-    collect_kv((2, 3), range(ns - 1, ns) if split else range(1, ns))
+    if split:
+        collect_kv((2,), range(ns - 1, ns))
+        weighed = [
+            weigh(kept_state(g), q_stack[1, g], g, True, True, late_id, far, 1)
+            for g in range(kv_heads)
+        ]
+        collect_kv((3,), range(ns - 1, ns))
+    else:
+        collect_kv((2, 3), range(1, ns))
     for g in range(kv_heads):
         if split:
-            state = attend(kept_state(g), q_stack[1, g], g, True, True, late_id, far, 1)
+            state = gather_values(weighed[g], g, True, far, 1)
         else:
             state = attend_all(kept_state(g), q_stack[1, g], g, True, True, late_id)
         store_attention(1, g, state)
         att_copy(1, g).start()
     project_side(1)
     finish_side(0)
+    finish_side(1)
     mixed[0] = norm_side(0)
-    finish_side(1)
     early_out, late_out = mixed[0], norm_side(1)
     swap = jnp.full(early_out.shape, swapped, jnp.int32) != 0
     out_ref[:block, :] = jnp.where(swap, late_out, early_out).astype(jnp.bfloat16)
     out_ref[block:, :] = jnp.where(swap, early_out, late_out).astype(jnp.bfloat16)
 
-    for chunk in range(4):
-        for distance in range(ns - 1):
-            for direction in range(2):
-                @pl.when(sends(direction, distance))
-                def _():
-                    kv_copy(direction, chunk, distance).wait_send()
-    for index in range(pairs):
-        w_copies(index)[1].wait_send()
-    for side in range(2):
-        for g in range(kv_heads):
-            att_copy(side, g).wait_send()
-        for step in range(1, pairs):
-            for piece in range(pieces):
-                part_copy(side, step, piece).wait_send()
-        for step in range(1, nh):
-            ssq_copy(side, step).wait_send()
+    for distance in range(ns - 1):
+        for direction in range(2):
+            @pl.when(sends(direction, distance))
+            def _():
+                if distance == 0:
+                    drain(kv.at[:, seq], kv_send.at[direction, distance])
+                else:
+                    @pl.when(bit == 0)
+                    def _():
+                        drain(kv.at[2:, seq], kv_send.at[direction, distance])
+
+                    @pl.when(bit == 1)
+                    def _():
+                        drain(kv.at[:, seq], kv_send.at[direction, distance])
+                        drain(peer_kv.at[:, seq], peer_send.at[direction, distance - 1])
+
+    @pl.when(bit == 1)
+    def _():
+        drain(kv.at[:2, : ns - 1], relay_send)
+    drain(w_peer, w_send)
+    drain(att, att_send)
+    if pairs > 1:
+        drain(part, part_send)
+    drain(ssq_in, ssq_send)
 
 
 def body(ns, nh, queries, keys, values, residual, weight, gain, order):
@@ -407,9 +537,10 @@
     return pl.pallas_call(
         functools.partial(kernel, ns, nh),
         out_shape=jax.ShapeDtypeStruct((rows, features), bf16),
-        in_specs=[pl.BlockSpec(memory_space=pltpu.SMEM)] + [hbm] * 6,
+        in_specs=[hbm] * 7,
         out_specs=vmem,
         scratch_shapes=[
+            pltpu.SMEM(order.shape, jnp.int32),
             pltpu.VMEM((rows, kv_width), bf16),
             pltpu.VMEM((rows, kv_width), bf16),
             pltpu.VMEM((features,), bf16),
@@ -430,18 +561,22 @@
             pltpu.VMEM((kv_heads, stack, 128), f32),
             pltpu.VMEM((2, block, features), f32),
             pltpu.VMEM((block, features), f32),
+            pltpu.VMEM((2, ns, block, kv_width), bf16),
+            dma((4,)),
             dma((3,)),
-            dma((2 + pairs,)),
-            dma((2, 4, ns)),
+            dma((2, ns - 1)),
             dma((4, ns)),
-            dma((pairs,)),
-            dma((pairs,)),
-            dma((2, kv_heads)),
-            dma((2, kv_heads)),
+            dma((2, max(ns - 2, 1))),
+            dma((2, ns)),
+            dma(()),
+            dma(()),
+            dma(()),
+            dma(()),
+            dma((2,)),
+            dma(()),
             dma((2, others, pieces)),
-            dma((2, others, pieces)),
-            dma((2, nh - 1)),
-            dma((2, nh - 1)),
+            dma(()),
+            dma((2,)),
         ],
         compiler_params=pltpu.CompilerParams(
             collective_id=0, has_side_effects=True, vmem_limit_bytes=40 * 1024 * 1024

time: 39.9 us -> 37.5 us (0.940)
  Pallas kernels: 38.9 us -> 36.5 us
    pallas_call x1, Pallas kernels: 38.9 us -> 36.5 us  [body(): pl.pallas_call(functools.partial(kernel, ns, nh), out_shape=jax.ShapeDtyp...]
where the time goes in v2:
time: 37.5 us; the launch traced here: 37.3 us
  Pallas kernels  36.5 us (97%)
  local copies, waits for them, and re-layouts  0.8 us (2%)
    pallas_call x1, Pallas kernels, body(): pl.pallas_call(functools.partial(kernel, ns, nh), out_shape=jax.ShapeDtyp...  36.5 us
    unnamed x1, local copies, waits for them, and re-layouts  0.8 us

profile of v2, /device:TPU:0, one launch (start us, length us, event | category | flops | bytes accessed | tf_op | source)
XLA Modules:
  0.0 37.3 jit_solution(2312281846616862920)
XLA Ops:
  0.0 36.5 %shard_map.73 = bf16[256,1024]{1,0:T(8,128)(2,1)S(1)} custom-call(s32[8]{0:T(128)} %order_hbm.1, bf16[256,256]{1,0:T(8,128)(2,1)} %k_hbm.1, bf16[256,256]{1,0:T(8,128)(2,1)} %v_hbm.1, bf16[1024]{0:T(1024)(128)(2,1)} %gain_hbm.1, bf16[256,1024]{1,0:T(8,128)(2,1)} %q_hbm.1, bf16[256,1024]{1,0:T(8,128)(2,1)} %res_hbm.1, bf16[1024,4096]{1,0:T(8,128)(2,1)} %w_hbm.1), custom_call_target="tpu_custom_call" | custom-call | tf_op jit(solution)/shard_map/pallas_call | solution.py:537
  36.5 0.8 %copy.9 = bf16[256,1024]{1,0:T(8,128)(2,1)} copy(bf16[256,1024]{1,0:T(8,128)(2,1)S(1)} %shard_map.73) | data formatting | bytes 1048576

commit v3 on v2

--- a/solution.py
+++ b/solution.py
@@ -235,14 +235,24 @@
         )
 
     w_pieces = list(range(pairs * slices))
-    at_once = 2
+    at_once = 4
 
     def w_next(count):
         for _ in range(min(count, len(w_pieces))):
-            w_remote(w_pieces.pop(0)).start()
+            number = w_pieces.pop(0)
+
+            @pl.when(bit == 1)
+            def _():
+                w_remote(number).start()
 
     for index in range(pairs):
         w_local(index).start()
+
+    @pl.when(bit == 0)
+    def _():
+        for number in w_pieces:
+            w_remote(number).start()
+
     w_next(at_once)
     res_copy.start()
 
@@ -254,21 +264,23 @@
                 :, h * HEAD_SIZE:(h + 1) * HEAD_SIZE
             ]
 
-    for distance in range(1, ns):
+    def pass_early(distance):
         for chunk in (0, 1):
             relay_kv(chunk, distance)
             if distance < ns - 1:
                 forward_kv(chunk, distance)
             w_next(1)
-        if distance == max(ns - 2, 1):
-            @pl.when(jnp.logical_not(edge))
-            def _():
-                start_kv(3)
+
+    for distance in range(1, max(ns - 1, 2)):
+        pass_early(distance)
+
+    @pl.when(jnp.logical_not(edge))
+    def _():
+        start_kv(3)
+
     if ns > 2:
-        for chunk in (2, 3):
-            forward_kv(chunk, 1, edges=True)
-    w_next(len(w_pieces))
-    collect_kv((0, 1), range(1, ns))
+        forward_kv(2, 1)
+        forward_kv(3, 1, edges=True)
 
     chunk_blocks = math.gcd(ns, 4)
     factor = math.log2(math.e) * HEAD_SIZE ** -0.5
@@ -294,16 +306,16 @@
             scores = (scores.reshape(group, block, chunk_keys) + bias[None]).reshape(
                 stack, chunk_keys
             )
-        top = jnp.max(scores, axis=1, keepdims=True)
+        top = jnp.broadcast_to(jnp.max(scores, axis=1, keepdims=True), (stack, HEAD_SIZE))
+        if state is not None:
+            top = jnp.maximum(state[0], top)
+        weights = jnp.exp2(scores - jnp.tile(top, (1, chunk_keys // HEAD_SIZE)))
+        total = jnp.broadcast_to(jnp.sum(weights, axis=1, keepdims=True), (stack, HEAD_SIZE))
         if state is None:
-            weights = jnp.exp2(scores - top)
-            return top, jnp.sum(weights, axis=1, keepdims=True), weights.astype(jnp.bfloat16), None
-        old_top, old_total, old_value = state
-        top = jnp.maximum(old_top, top)
-        weights = jnp.exp2(scores - top)
-        scale = jnp.exp2(old_top - top)
-        total = old_total * scale + jnp.sum(weights, axis=1, keepdims=True)
-        return top, total, weights.astype(jnp.bfloat16), old_value * scale
+            return top, total, weights.astype(jnp.bfloat16), None
+        scale = jnp.exp2(state[0] - top)
+        total = state[1] * scale + total
+        return top, total, weights.astype(jnp.bfloat16), state[2] * scale
 
     def gather_values(weighed, g, late, at, blocks):
         top, total, weights, value = weighed
@@ -321,8 +333,8 @@
             return attend(state, q, g, late, masked, own_id, 0, ns)
         if state is None:
             state = (
-                jnp.full((stack, 1), MASKED, jnp.float32),
-                jnp.zeros((stack, 1), jnp.float32),
+                jnp.full((stack, HEAD_SIZE), MASKED, jnp.float32),
+                jnp.zeros((stack, HEAD_SIZE), jnp.float32),
                 jnp.zeros((stack, HEAD_SIZE), jnp.float32),
             )
         return lax.fori_loop(
@@ -381,25 +393,52 @@
 
     spans = [slice(i * piece_width, (i + 1) * piece_width) for i in range(pieces)]
 
-    def project_side(side):
-        owner = lax.rem(pair + 1, pairs)
+    def lead(side, owner):
         for columns in spans:
             ahead[:, columns] = own_part(side, owner, columns)
         drain(peer_att.at[side], att_recv.at[side])
+
+    def project_others(side, first):
+        if first:
+            lead(side, lax.rem(pair + 1, pairs))
         for step in range(1, pairs):
             owner = lax.rem(pair + step, pairs)
             for piece, columns in enumerate(spans):
-                own = ahead[:, columns] if step == 1 else own_part(side, owner, columns)
+                led = first and step == 1
+                own = ahead[:, columns] if led else own_part(side, owner, columns)
                 part[side, step - 1, piece] = (own + peer_part(side, owner, columns)).astype(
                     jnp.bfloat16
                 )
                 part_copy(side, step, piece).start()
+
+    def project_mine(side, first):
+        if first:
+            lead(side, pair)
         for columns in spans:
+            own = ahead[:, columns] if first else own_part(side, pair, columns)
             mixed[side, :, columns] = (
-                own_part(side, pair, columns)
-                + peer_part(side, pair, columns)
-                + own_residual(side, columns)
+                own + peer_part(side, pair, columns) + own_residual(side, columns)
             )
+
+    def project_side(side, stagger, between=None):
+        def others_first():
+            project_others(side, pairs > 1)
+            if between is not None:
+                between()
+            project_mine(side, pairs == 1)
+
+        if not stagger:
+            others_first()
+            return
+
+        @pl.when(bit == 0)
+        def _():
+            others_first()
+
+        @pl.when(bit == 1)
+        def _():
+            project_mine(side, True)
+            project_others(side, False)
 
     def ssq_copy(side, step):
         return pltpu.make_async_remote_copy(
@@ -440,33 +479,70 @@
     def keep_state(g, state):
         top, total, value = state
         acc[g] = value
-        peak[g] = jnp.broadcast_to(top, (stack, 128))
-        denom[g] = jnp.broadcast_to(total, (stack, 128))
+        peak[g] = top
+        denom[g] = total
 
     def kept_state(g):
-        return peak[g][:, :1], denom[g][:, :1], acc[g]
+        return peak[g], denom[g], acc[g]
 
     late_steps = list(range(1, ns - 1))
-    for g in range(kv_heads):
-        store_attention(0, g, attend_all(None, q_stack[0, g], g, False, True, early_id))
-        att_copy(0, g).start()
-    for g in range(kv_heads):
-        keep_state(g, attend_all(None, q_stack[1, g], g, False, False, late_id))
-    for distance in late_steps[:1]:
-        for chunk in (2, 3):
-            forward_kv(chunk, distance, edges=False)
+    split = ns == chunk_blocks and ns > 2
+    heads = range(kv_heads)
+    if split:
+        lower = seq < ns // 2
+        begin, far = jnp.where(lower, 0, 1), jnp.where(lower, ns - 1, 0)
+        collect_kv((0, 1), range(1, ns - 1))
+        early = [
+            attend(None, q_stack[0, g], g, False, True, early_id, begin, ns - 1) for g in heads
+        ]
+        for g in heads:
+            keep_state(g, attend(None, q_stack[1, g], g, False, False, late_id, begin, ns - 1))
+        relay_kv(0, ns - 1)
+        w_next(1)
+        collect_kv((0,), range(ns - 1, ns))
+        weighed = [
+            weigh(early[g], q_stack[0, g], g, False, True, early_id, far, 1) for g in heads
+        ]
+        relay_kv(1, ns - 1)
+        w_next(len(w_pieces))
+        collect_kv((1,), range(ns - 1, ns))
+        for g in heads:
+            store_attention(0, g, gather_values(weighed[g], g, False, far, 1))
+            att_copy(0, g).start()
+        forward_kv(3, 1, edges=False)
+        for g in heads:
+            keep_state(
+                g, attend(kept_state(g), q_stack[1, g], g, False, False, late_id, far, 1)
+            )
+    else:
+        if ns > 2:
+            pass_early(ns - 1)
+        w_next(len(w_pieces))
+        collect_kv((0, 1), range(1, ns))
+        for g in heads:
+            store_attention(0, g, attend_all(None, q_stack[0, g], g, False, True, early_id))
+            att_copy(0, g).start()
+        for g in heads:
+            keep_state(g, attend_all(None, q_stack[1, g], g, False, False, late_id))
+    if ns > 2 and not split:
+        forward_kv(3, 1, edges=False)
+    if split:
+        for distance in late_steps[1:]:
+            for chunk in (2, 3):
+                forward_kv(chunk, distance)
     drain(w_own, local_sem.at[2])
     drain(w_peer, w_recv)
     res_copy.wait()
     loads[2].wait()
-    project_side(0)
-    for distance in late_steps[1:]:
-        for chunk in (2, 3):
-            forward_kv(chunk, distance)
-    split = ns == chunk_blocks and ns > 1
+
+    def late_forwards():
+        if not split:
+            for distance in late_steps[1:]:
+                for chunk in (2, 3):
+                    forward_kv(chunk, distance)
+
+    project_side(0, False, late_forwards)
     if split:
-        lower = seq < ns // 2
-        begin, far = jnp.where(lower, 0, 1), jnp.where(lower, ns - 1, 0)
         collect_kv((2, 3), range(1, ns - 1))
         for g in range(kv_heads):
             keep_state(
@@ -488,7 +564,7 @@
             state = attend_all(kept_state(g), q_stack[1, g], g, True, True, late_id)
         store_attention(1, g, state)
         att_copy(1, g).start()
-    project_side(1)
+    project_side(1, False)
     finish_side(0)
     finish_side(1)
     mixed[0] = norm_side(0)

time: 37.5 us -> 36.1 us (0.963)
  Pallas kernels: 36.5 us -> 35.2 us
    pallas_call x1, Pallas kernels: 36.5 us -> 35.2 us  [body(): pl.pallas_call(functools.partial(kernel, ns, nh), out_shape=jax.ShapeDtyp...]
where the time goes in v3:
time: 36.1 us; the launch traced here: 36 us
  Pallas kernels  35.2 us (98%)
  local copies, waits for them, and re-layouts  0.8 us (2%)
    pallas_call x1, Pallas kernels, body(): pl.pallas_call(functools.partial(kernel, ns, nh), out_shape=jax.ShapeDtyp...  35.2 us
    unnamed x1, local copies, waits for them, and re-layouts  0.8 us

profile of v3, /device:TPU:0, one launch (start us, length us, event | category | flops | bytes accessed | tf_op | source)
XLA Modules:
  0.0 36.0 jit_solution(7003217902008982318)
XLA Ops:
  0.0 35.2 %shard_map.73 = bf16[256,1024]{1,0:T(8,128)(2,1)S(1)} custom-call(s32[8]{0:T(128)} %order_hbm.1, bf16[256,256]{1,0:T(8,128)(2,1)} %k_hbm.1, bf16[256,256]{1,0:T(8,128)(2,1)} %v_hbm.1, bf16[1024]{0:T(1024)(128)(2,1)} %gain_hbm.1, bf16[256,1024]{1,0:T(8,128)(2,1)} %q_hbm.1, bf16[256,1024]{1,0:T(8,128)(2,1)} %res_hbm.1, bf16[1024,4096]{1,0:T(8,128)(2,1)} %w_hbm.1), custom_call_target="tpu_custom_call" | custom-call | tf_op jit(solution)/shard_map/pallas_call | solution.py:613
  35.2 0.8 %copy.9 = bf16[256,1024]{1,0:T(8,128)(2,1)} copy(bf16[256,1024]{1,0:T(8,128)(2,1)S(1)} %shard_map.73) | data formatting | bytes 1048576

commit v4 on v3

--- a/solution.py
+++ b/solution.py
@@ -18,7 +18,7 @@
     ns, nh, order_hbm, k_hbm, v_hbm, gain_hbm, q_hbm, res_hbm, w_hbm, out_ref,
     order_ref, k_ref, v_ref, gain_ref, q_vm, res_vm, q_stack, w_own, w_peer, kv, att, peer_att, part, part_in,
     ssq, ssq_in, acc, peak, denom, mixed, ahead, peer_kv,
-    load_sem, local_sem, kv_send, kv_recv, peer_send, peer_recv, relay_send, w_send, w_recv, att_send, att_recv,
+    load_sem, local_sem, kv_send, kv_recv, peer_recv, relay_send, w_send, w_recv, att_send, att_recv,
     part_send, part_recv, ssq_send, ssq_recv,
 ):
     seq, head = lax.axis_index("seq"), lax.axis_index("head")
@@ -98,7 +98,7 @@
             src_ref=kv.at[chunk, piece],
             dst_ref=kv.at[chunk, piece],
             send_sem=kv_send.at[direction, distance],
-            recv_sem=kv_recv.at[chunk, piece],
+            recv_sem=kv_recv.at[chunk, piece - direction],
             device_id={"seq": target},
             device_id_type=MESH,
         )
@@ -116,7 +116,7 @@
             src_ref=kv.at[chunk, seq],
             dst_ref=peer_kv.at[chunk, seq],
             send_sem=kv_send.at[direction, 0],
-            recv_sem=peer_recv.at[chunk, seq],
+            recv_sem=peer_recv.at[chunk, seq - direction],
             device_id={"seq": seq + 1 if direction == 0 else seq - 1, "head": sibling},
             device_id_type=MESH,
         )
@@ -127,8 +127,8 @@
         return pltpu.make_async_remote_copy(
             src_ref=peer_kv.at[chunk, piece],
             dst_ref=peer_kv.at[chunk, piece],
-            send_sem=peer_send.at[direction, distance - 1],
-            recv_sem=peer_recv.at[chunk, piece],
+            send_sem=kv_send.at[direction, distance],
+            recv_sem=peer_recv.at[chunk, piece - direction],
             device_id={"seq": seq + 1 if direction == 0 else seq - 1},
             device_id_type=MESH,
         )
@@ -142,7 +142,7 @@
             src_ref=peer_kv.at[chunk, piece],
             dst_ref=kv.at[chunk, piece],
             send_sem=relay_send,
-            recv_sem=kv_recv.at[chunk, piece],
+            recv_sem=kv_recv.at[chunk, piece - direction],
             device_id={"head": sibling},
             device_id_type=MESH,
         )
@@ -208,11 +208,12 @@
                         kv_copy(direction, chunk, distance).wait_recv()
 
     edge = jnp.logical_or(seq == 0, seq == ns - 1)
-    for chunk in (0, 1, 2):
+    for chunk in (0, 1):
         start_kv(chunk)
 
     @pl.when(edge)
     def _():
+        start_kv(2)
         start_kv(3)
 
     def w_local(index):
@@ -276,6 +277,7 @@
 
     @pl.when(jnp.logical_not(edge))
     def _():
+        start_kv(2)
         start_kv(3)
 
     if ns > 2:
@@ -364,7 +366,7 @@
             device_id_type=MESH,
         )
 
-    pieces = features // math.gcd(features, 256)
+    pieces = features // math.gcd(features, 512)
     piece_width = features // pieces
 
     def part_copy(side, step, piece):
@@ -372,7 +374,7 @@
             src_ref=part.at[side, step - 1, piece],
             dst_ref=part_in.at[side, step - 1, piece],
             send_sem=part_send,
-            recv_sem=part_recv.at[side, step - 1, piece],
+            recv_sem=part_recv.at[step - 1, 0 if side == 0 else 1 + piece],
             device_id={"head": 2 * lax.rem(pair + step, pairs) + bit},
             device_id_type=MESH,
         )
@@ -452,10 +454,14 @@
 
     def finish_side(side):
         squares = jnp.zeros((block, 128), jnp.float32)
+        if side == 0:
+            for step in range(1, pairs):
+                drain(part_in.at[side, step - 1], part_recv.at[step - 1, 0])
         for piece, columns in enumerate(spans):
             total = mixed[side, :, columns]
             for step in range(1, pairs):
-                part_copy(side, step, piece).wait_recv()
+                if side == 1:
+                    part_copy(side, step, piece).wait_recv()
                 total = total + part_in[side, step - 1, piece].astype(jnp.float32)
             mixed[side, :, columns] = total
             for lane in range(0, piece_width, 128):
@@ -495,8 +501,6 @@
         early = [
             attend(None, q_stack[0, g], g, False, True, early_id, begin, ns - 1) for g in heads
         ]
-        for g in heads:
-            keep_state(g, attend(None, q_stack[1, g], g, False, False, late_id, begin, ns - 1))
         relay_kv(0, ns - 1)
         w_next(1)
         collect_kv((0,), range(ns - 1, ns))
@@ -511,9 +515,7 @@
             att_copy(0, g).start()
         forward_kv(3, 1, edges=False)
         for g in heads:
-            keep_state(
-                g, attend(kept_state(g), q_stack[1, g], g, False, False, late_id, far, 1)
-            )
+            keep_state(g, attend_all(None, q_stack[1, g], g, False, False, late_id))
     else:
         if ns > 2:
             pass_early(ns - 1)
@@ -586,8 +588,7 @@
 
                     @pl.when(bit == 1)
                     def _():
-                        drain(kv.at[:, seq], kv_send.at[direction, distance])
-                        drain(peer_kv.at[:, seq], peer_send.at[direction, distance - 1])
+                        drain(kv.at[:3, :2], kv_send.at[direction, distance])
 
     @pl.when(bit == 1)
     def _():
@@ -607,7 +608,7 @@
     features = residual.shape[1]
     pairs = nh // 2
     others = max(pairs - 1, 1)
-    pieces = features // math.gcd(features, 256)
+    pieces = features // math.gcd(features, 512)
     vmem, hbm = pl.BlockSpec(memory_space=pltpu.VMEM), pl.BlockSpec(memory_space=pl.ANY)
     bf16, f32, dma = jnp.bfloat16, jnp.float32, pltpu.SemaphoreType.DMA
     return pl.pallas_call(
@@ -641,16 +642,15 @@
             dma((4,)),
             dma((3,)),
             dma((2, ns - 1)),
-            dma((4, ns)),
-            dma((2, max(ns - 2, 1))),
-            dma((2, ns)),
+            dma((4, ns - 1)),
+            dma((2, ns - 1)),
             dma(()),
             dma(()),
             dma(()),
             dma(()),
             dma((2,)),
             dma(()),
-            dma((2, others, pieces)),
+            dma((others, 1 + pieces)),
             dma(()),
             dma((2,)),
         ],

time: 36.1 us -> 36 us (level)
  no operation moved by 1% of the time
where the time goes in v4:
time: 36 us; the launch traced here: 35.8 us
  Pallas kernels  35 us (97%)
  local copies, waits for them, and re-layouts  0.8 us (2%)
    pallas_call x1, Pallas kernels, body(): pl.pallas_call(functools.partial(kernel, ns, nh), out_shape=jax.ShapeDtyp...  35 us
    unnamed x1, local copies, waits for them, and re-layouts  0.8 us

profile of v4, /device:TPU:0, one launch (start us, length us, event | category | flops | bytes accessed | tf_op | source)
XLA Modules:
  0.0 35.8 jit_solution(2872213881100383266)
XLA Ops:
  0.0 35.0 %shard_map.73 = bf16[256,1024]{1,0:T(8,128)(2,1)S(1)} custom-call(s32[8]{0:T(128)} %order_hbm.1, bf16[256,256]{1,0:T(8,128)(2,1)} %k_hbm.1, bf16[256,256]{1,0:T(8,128)(2,1)} %v_hbm.1, bf16[1024]{0:T(1024)(128)(2,1)} %gain_hbm.1, bf16[256,1024]{1,0:T(8,128)(2,1)} %q_hbm.1, bf16[256,1024]{1,0:T(8,128)(2,1)} %res_hbm.1, bf16[1024,4096]{1,0:T(8,128)(2,1)} %w_hbm.1), custom_call_target="tpu_custom_call" | custom-call | tf_op jit(solution)/shard_map/pallas_call | solution.py:614
  35.0 0.8 %copy.9 = bf16[256,1024]{1,0:T(8,128)(2,1)} copy(bf16[256,1024]{1,0:T(8,128)(2,1)S(1)} %shard_map.73) | data formatting | bytes 1048576
